TPU v7x, 32 devices: a whole 2x2x4 slice. The times are simulated.
32 devices in a mesh: row: 4 (over y, x), col: 8 (over z, core).
Axes of the slice: x: 2, y: 2, z: 4, core: 2. Of those that a mesh axis runs over, the one named last changes fastest.
Arguments:
- out_grad: bfloat16 [4096, 512], P('col', 'row'), may hold values from -6 to 6
- node_in: bfloat16 [4096, 512], P(('row', 'col')), may hold values from -0.09375 to 0.09375
- weights: bfloat16 [3, 512, 512], replicated, may hold values from -0.25 to 0.25
- tile_vals: bfloat16 [3, 8, 4, 32, 128, 128], P(None, 'col', 'row'), may hold values from -0.15625 to 0.15625
- tile_rows: int32 [3, 8, 4, 32], P(None, 'col', 'row'), may hold values from 0 to 3
- tile_cols: int32 [3, 8, 4, 32], P(None, 'col', 'row'), may hold values from 0 to 7
- tile_count: int32 [3, 8, 4], P(None, 'col', 'row'), may hold values from 1 to 32, as said below
Outputs:
- d_nodes: bfloat16 [4096, 512], P(('row', 'col'))
- d_weights: float32 [3, 512, 512], replicated
Inputs may be any that keep to these rules, and one draw needn't show every extreme that they name: Only the first tile_count slots of a block's list hold tiles; later slots are ignored. In every relation some block uses all 32 slots. `tile_rows`: coordinates may repeat within a block's list; such tiles add.
All inputs are finite; a program needn't handle non-finite values.
Results may differ from a plain program's by a relative error of at most 0.005.
Values may be sent and summed in bfloat16 or wider, within the bound.
A program may use at most 256 MiB of HBM per device.

v0:
```python
import jax
import jax.numpy as jnp
from jax import lax
from jax.sharding import PartitionSpec as P

group_width = 8


def weight_terms(inputs, sums):
    high_part = sums.astype(jnp.bfloat16)
    low_part = (sums - high_part.astype(jnp.float32)).astype(jnp.bfloat16)
    first = jnp.einsum("nd,rne->rde", inputs, high_part, preferred_element_type=jnp.float32)
    second = jnp.einsum("nd,rne->rde", inputs, low_part, preferred_element_type=jnp.float32)
    return first + second


def tile_sums(tile_block, row_ids, col_ids, count_now, operand, relation, initial, relations):
    tile_size = tile_block.shape[-1]
    feature_width = operand.shape[1] // 2

    def group_step(group_index, partial_stack):
        first_slot = group_index * group_width
        for offset in range(group_width):
            slot_index = first_slot + offset
            values = lax.dynamic_index_in_dim(tile_block, slot_index, 0, keepdims=False)
            source = lax.dynamic_slice_in_dim(
                operand, row_ids[slot_index] * tile_size, tile_size, 0
            )
            product = lax.dot_general(
                values, source, (((0,), (0,)), ((), ())), preferred_element_type=jnp.float32
            )
            product = jnp.where(slot_index < count_now, product, 0.0)
            target = col_ids[slot_index] * tile_size
            own_part = lax.dynamic_slice(
                partial_stack, (relation, target, 0), (1, tile_size, feature_width)
            )
            partial_stack = lax.dynamic_update_slice(
                partial_stack, own_part + product[None, :, :feature_width], (relation, target, 0)
            )
            mixed_part = lax.dynamic_slice(
                partial_stack, (relations, target, 0), (1, tile_size, feature_width)
            )
            partial_stack = lax.dynamic_update_slice(
                partial_stack, mixed_part + product[None, :, feature_width:], (relations, target, 0)
            )
        return partial_stack

    group_count = (count_now + group_width - 1) // group_width
    return lax.fori_loop(0, group_count, group_step, initial)


def body(out_grad, node_in, weights, tile_vals, tile_rows, tile_cols, tile_count):
    grad_block = lax.all_gather(out_grad, "row", axis=1, tiled=True)
    relations = weights.shape[0]
    feature_width = weights.shape[1]
    source_rows = node_in.shape[0] * lax.axis_size("col")
    partial_stack = jnp.zeros((relations + 1, source_rows, feature_width), jnp.float32)
    for relation in range(relations):
        premixed = lax.dot_general(
            grad_block,
            weights[relation],
            (((1,), (1,)), ((), ())),
            preferred_element_type=jnp.float32,
        ).astype(jnp.bfloat16)
        operand = jnp.concatenate([grad_block, premixed], axis=1)
        partial_stack = tile_sums(
            tile_vals[relation, 0, 0],
            tile_rows[relation, 0, 0],
            tile_cols[relation, 0, 0],
            tile_count[relation, 0, 0],
            operand,
            relation,
            partial_stack,
            relations,
        )
    reduced = lax.psum_scatter(partial_stack[relations], "col", scatter_dimension=0, tiled=True)
    d_nodes = reduced.astype(jnp.bfloat16)
    piece = lax.all_gather(node_in, "col", axis=0, tiled=True)
    sums_here = lax.dynamic_slice(
        partial_stack, (0, 0, 0), (relations, piece.shape[0], feature_width)
    )
    local_grads = weight_terms(piece, sums_here)
    d_weights = lax.psum(local_grads, ("row", "col"))
    return (d_nodes, d_weights)


def solution(mesh):
    return jax.shard_map(
        body,
        mesh=mesh,
        in_specs=(
            P("col", "row"),
            P(("row", "col"), None),
            P(),
            P(None, "col", "row", None, None, None),
            P(None, "col", "row", None),
            P(None, "col", "row", None),
            P(None, "col", "row"),
        ),
        out_specs=(P(("row", "col"), None), P()),
        check_vma=False,
    )
```

profile of v0, /device:TPU:0, one launch (start us, length us, event | category | flops | bytes accessed | tf_op | source)
XLA Modules:
  0.0 781.8 jit_solution(16126669114292662267)
XLA Ops:
  10.9 11.5 %all_gather.6 = bf16[512,512]{0,1:T(8,128)(2,1)S(1)} all-gather(bf16[512,128]{0,1:T(8,128)(2,1)S(1)} %copy.9), channel_id=1, replica_groups=mesh['row'=4,'col'=8] {'row'}, dimensions={1}, use_global_device_ids=true | all-gather | bytes 655360 | tf_op jit(solution)/shard_map/all_gather | solution.py:53
  30.3 3.6 slice_bitcast_fusion.49
  34.0 4.3 broadcast_in_dim.331
  38.3 50.7 %while.36 = (s32[]{:T(128)}, f32[4,1024,512]{2,1,0:T(8,128)}, s32[]{:T(128)}, s32[32]{0:T(128)S(1)}, s32[]{:T(128)}, /*index=5*/bf16[32,128,128]{2,1,0:T(8,128)(...) while((s32[]{:T(128)}, f32[4,1024,512]{2,1,0:T(8,128)}, ...), condition=%wide.region_1.2_spmd, body=%wide.region_0.1_spmd.sunk | while | flops 270532640 | bytes 19138228 | solution.py:49
  41.9 1.7 fusion.328
  48.1 1.7 fusion.330
  54.4 1.7 fusion.332
  60.6 1.7 fusion.334
  62.4 1.7 fusion.335
  73.2 1.7 fusion.338
  79.4 1.7 fusion.340
  81.1 1.7 fusion.341
  90.5 151.8 %while.37 = (s32[]{:T(128)}, f32[4,1024,512]{2,1,0:T(8,128)}, s32[]{:T(128)}, s32[32]{0:T(128)S(1)}, s32[]{:T(128)}, /*index=5*/bf16[32,128,128]{2,1,0:T(8,128)(...) while((s32[]{:T(128)}, f32[4,1024,512]{2,1,0:T(8,128)}, ...), condition=%wide.region_3.4_spmd, body=%wide.region_2.3_spmd.sunk | while | flops 270532640 | bytes 19138228 | solution.py:49
  94.1 1.7 fusion.361
  100.2 1.7 fusion.363
  101.9 1.7 fusion.364
  106.4 1.7 fusion.365
  112.7 1.7 fusion.367
  126.9 1.7 fusion.372
  133.1 1.7 fusion.374
  137.7 1.7 fusion.375
  139.4 1.7 fusion.376
  144.6 1.7 fusion.361
  146.3 1.7 fusion.362
  152.4 1.7 fusion.364
  156.9 1.7 fusion.365
  158.6 1.7 fusion.366
  163.3 1.7 fusion.367
  165.0 1.7 fusion.368
  175.8 1.7 fusion.371
  177.5 1.7 fusion.372
  182.0 1.7 fusion.373
  183.7 1.7 fusion.374
  188.3 1.7 fusion.375
  190.0 1.7 fusion.376
  195.2 1.7 fusion.361
  196.9 1.7 fusion.362
  201.4 1.7 fusion.363
  203.1 1.7 fusion.364
  207.6 1.7 fusion.365
  213.9 1.7 fusion.367
  220.1 1.7 fusion.369
  226.4 1.7 fusion.371
  228.1 1.7 fusion.372
  240.5 1.7 fusion.376
  243.7 45.3 %while.38 = (s32[]{:T(128)}, f32[4,1024,512]{2,1,0:T(8,128)}, s32[]{:T(128)}, s32[32]{0:T(128)S(1)}, s32[]{:T(128)}, /*index=5*/bf16[32,128,128]{2,1,0:T(8,128)(...) while((s32[]{:T(128)}, f32[4,1024,512]{2,1,0:T(8,128)}, ...), condition=%wide.region_5.6_spmd, body=%wide.region_4.5_spmd.sunk | while | flops 270532640 | bytes 19138228 | solution.py:49
  246.7 1.7 fusion.394
  248.4 1.7 fusion.395
  252.3 1.7 fusion.396
  257.8 1.7 fusion.398
  265.2 1.7 fusion.401
  270.7 1.7 fusion.403
  274.5 1.7 fusion.404
  280.1 1.7 fusion.406
  281.8 1.7 fusion.407
  285.6 1.7 fusion.408
  287.3 1.7 fusion.409
  289.0 8.7 %copy.13 = f32[4,1024,512]{1,2,0:T(8,128)} copy(f32[4,1024,512]{2,1,0:T(8,128)} %get-tuple-element.334) | data formatting | bytes 16777216 | tf_op jit(solution)/shard_map/while | solution.py:49
  297.7 5.0 fusion.193
  303.4 3.5 add_bitcast_fusion
  307.0 3.2 slice_bitcast_fusion.48
  310.2 426.4 %all-reduce.2.cloned.1.call-done = f32[3,512,512]{1,2,0:T(8,128)} async-done(((f32[3,512,512]{1,2,0:T(8,128)}), f32[3,512,512]{1,2,0:T(8,128)}) %all-reduce.2.cloned.1.call-update) | async-done | bytes 3145744 | tf_op jit(solution)/shard_map/psum | solution.py:83
  736.6 3.5 copy.14
  740.1 33.6 %reduce-scatter.2.cloned.1.call-done = f32[128,512]{1,0:T(8,128)} async-done(((f32[1024,512]{1,0:T(8,128)}), f32[128,512]{1,0:T(8,128)}) %reduce-scatter.2.cloned.1.call-update) | async-done | bytes 262160 | tf_op jit(solution)/shard_map/reduce_scatter | solution.py:76
  (100 shorter events, 101.8 us)
Async XLA Ops:
  7.2 290.5 %all-gather.2.cloned.1.call-start = ((), (), s32[]{:S(2)}) async-start(), calls=%async_computation.2 | async-start | bytes 1179648 | tf_op jit(solution)/shard_map/all_gather | solution.py:78
  7.9 728.7 %all-reduce.2.cloned.1.call-start = ((), (), s32[]{:S(2)}) async-start(), calls=%async_computation.3 | async-start | bytes 6291456 | tf_op jit(solution)/shard_map/psum | solution.py:83
  23.9 10.1 %copy-start.1 = (s32[3,1,1,32]{3,2,1,0:T(1,128)S(1)}, s32[3,1,1,32]{3,2,1,0:T(1,128)}, u32[]{:S(2)}) copy-start(s32[3,1,1,32]{3,2,1,0:T(1,128)} %param.17) | copy-start | bytes 1156
  23.9 10.0 %copy-start.2 = (s32[3,1,1,32]{3,2,1,0:T(1,128)S(1)}, s32[3,1,1,32]{3,2,1,0:T(1,128)}, u32[]{:S(2)}) copy-start(s32[3,1,1,32]{3,2,1,0:T(1,128)} %param.18) | copy-start | bytes 1156
  297.7 5.5 copy-start
  297.7 5.7 copy-start.3
  306.9 466.8 %reduce-scatter.2.cloned.1.call-start = ((), (), s32[]{:S(2)}) async-start(), calls=%async_computation.1 | async-start | bytes 2359296 | tf_op jit(solution)/shard_map/reduce_scatter | solution.py:76
Sparse Core Ops, SparseCore 0:
  9.6 24.9 all-gather.1
  307.0 429.4 all-reduce.1
  738.9 34.7 reduce-scatter.1
where the time goes:
time: 794 us; the launch traced here: 782 us
  waiting for transfers between devices  461 us (58%)
  other arithmetic  139 us (18%)
  loops' own time  74.2 us (9%)
  matrix products  47.2 us (6%)
  local copies, waits for them, and re-layouts  33.6 us (4%)
  between operations  15.7 us (2%)
  blocking collectives  11.5 us (1%)
    psum x1, waiting for transfers between devices, body(): d_weights = lax.psum(local_grads, ('row', 'col'))  426 us
    another operation x3, loops' own time, tile_sums(): return lax.fori_loop(0, group_count, group_step, initial)  74.2 us
    dynamic_update_slice x40, other arithmetic, group_step(): lax.dynamic_update_slice(partial_stack, own_part + product[None, :, :feat...  67.9 us
    dynamic_update_slice x40, other arithmetic, group_step(): lax.dynamic_update_slice(partial_stack, mixed_part + product[None, :, fea...  67.8 us
    dot_general x40, matrix products, group_step(): lax.dot_general(values, source, (((0,), (0,)), ((), ())), preferred_eleme...  34.3 us
    reduce_scatter x1, waiting for transfers between devices, body(): lax.psum_scatter(partial_stack[relations], 'col', scatter_dimension=0, ti...  33.6 us
  transfers between devices with their start and end apart: 3, of which 2 were waited for; matrix products, arithmetic and copies ran while one was open for 27% of the time, Pallas kernels for 0%

commit v1 on v0

--- a/solution.py
+++ b/solution.py
@@ -80,7 +80,8 @@
         partial_stack, (0, 0, 0), (relations, piece.shape[0], feature_width)
     )
     local_grads = weight_terms(piece, sums_here)
-    d_weights = lax.psum(local_grads, ("row", "col"))
+    one_axis = lax.psum(local_grads, "col")
+    d_weights = lax.psum(one_axis, "row")
     return (d_nodes, d_weights)
 
 

time: 794 us -> 825 us (1.039)
  waiting for transfers between devices: 461 us -> 491 us
    psum x1 -> x2, waiting for transfers between devices: 426 us -> 452 us  [the longest x1 365 us: body(): one_axis = lax.psum(local_grads, 'col')]
  transfers between devices with their start and end apart: 3 -> 4, of which waited for: 2 -> 3; matrix products, arithmetic and copies ran while one was open for 27% -> 25% of each run, Pallas kernels for 0% -> 0%
where the time goes in v1:
time: 825 us; the launch traced here: 812 us
  waiting for transfers between devices  491 us (60%)
  other arithmetic  139 us (17%)
  loops' own time  74.2 us (9%)
  matrix products  47.2 us (6%)
  local copies, waits for them, and re-layouts  33.6 us (4%)
  between operations  15.7 us (2%)
  blocking collectives  11.5 us (1%)
    psum x1, waiting for transfers between devices, body(): one_axis = lax.psum(local_grads, 'col')  365 us
    psum x1, waiting for transfers between devices, body(): d_weights = lax.psum(one_axis, 'row')  86.9 us
    another operation x3, loops' own time, tile_sums(): return lax.fori_loop(0, group_count, group_step, initial)  74.2 us
    dynamic_update_slice x40, other arithmetic, group_step(): lax.dynamic_update_slice(partial_stack, own_part + product[None, :, :feat...  67.9 us
    dynamic_update_slice x40, other arithmetic, group_step(): lax.dynamic_update_slice(partial_stack, mixed_part + product[None, :, fea...  67.8 us
    reduce_scatter x1, waiting for transfers between devices, body(): lax.psum_scatter(partial_stack[relations], 'col', scatter_dimension=0, ti...  38.2 us
    dot_general x40, matrix products, group_step(): lax.dot_general(values, source, (((0,), (0,)), ((), ())), preferred_eleme...  34.3 us
  transfers between devices with their start and end apart: 4, of which 3 were waited for; matrix products, arithmetic and copies ran while one was open for 25% of the time, Pallas kernels for 0%

profile of v1, /device:TPU:0, one launch (start us, length us, event | category | flops | bytes accessed | tf_op | source)
XLA Modules:
  0.0 812.1 jit_solution(1025831593036590659)
XLA Ops:
  10.9 11.5 %all_gather.6 = bf16[512,512]{0,1:T(8,128)(2,1)S(1)} all-gather(bf16[512,128]{0,1:T(8,128)(2,1)S(1)} %copy.9), channel_id=1, replica_groups=mesh['row'=4,'col'=8] {'row'}, dimensions={1}, use_global_device_ids=true | all-gather | bytes 655360 | tf_op jit(solution)/shard_map/all_gather | solution.py:53
  30.3 3.6 slice_bitcast_fusion.49
  34.0 4.3 broadcast_in_dim.331
  38.3 50.7 %while.36 = (s32[]{:T(128)}, f32[4,1024,512]{2,1,0:T(8,128)}, s32[]{:T(128)}, s32[32]{0:T(128)S(1)}, s32[]{:T(128)}, /*index=5*/bf16[32,128,128]{2,1,0:T(8,128)(...) while((s32[]{:T(128)}, f32[4,1024,512]{2,1,0:T(8,128)}, ...), condition=%wide.region_1.2_spmd, body=%wide.region_0.1_spmd.sunk | while | flops 270532640 | bytes 19138228 | solution.py:49
  41.9 1.7 fusion.328
  48.1 1.7 fusion.330
  60.6 1.7 fusion.334
  62.4 1.7 fusion.335
  73.2 1.7 fusion.338
  79.4 1.7 fusion.340
  81.1 1.7 fusion.341
  90.5 151.8 %while.37 = (s32[]{:T(128)}, f32[4,1024,512]{2,1,0:T(8,128)}, s32[]{:T(128)}, s32[32]{0:T(128)S(1)}, s32[]{:T(128)}, /*index=5*/bf16[32,128,128]{2,1,0:T(8,128)(...) while((s32[]{:T(128)}, f32[4,1024,512]{2,1,0:T(8,128)}, ...), condition=%wide.region_3.4_spmd, body=%wide.region_2.3_spmd.sunk | while | flops 270532640 | bytes 19138228 | solution.py:49
  94.1 1.7 fusion.361
  100.2 1.7 fusion.363
  101.9 1.7 fusion.364
  106.4 1.7 fusion.365
  112.7 1.7 fusion.367
  126.9 1.7 fusion.372
  133.1 1.7 fusion.374
  137.7 1.7 fusion.375
  139.4 1.7 fusion.376
  144.6 1.7 fusion.361
  146.3 1.7 fusion.362
  152.4 1.7 fusion.364
  156.9 1.7 fusion.365
  158.6 1.7 fusion.366
  163.3 1.7 fusion.367
  165.0 1.7 fusion.368
  175.8 1.7 fusion.371
  177.5 1.7 fusion.372
  182.0 1.7 fusion.373
  183.7 1.7 fusion.374
  188.3 1.7 fusion.375
  190.0 1.7 fusion.376
  195.2 1.7 fusion.361
  196.9 1.7 fusion.362
  201.4 1.7 fusion.363
  203.1 1.7 fusion.364
  207.6 1.7 fusion.365
  213.9 1.7 fusion.367
  220.1 1.7 fusion.369
  226.4 1.7 fusion.371
  228.1 1.7 fusion.372
  240.5 1.7 fusion.376
  243.7 45.3 %while.38 = (s32[]{:T(128)}, f32[4,1024,512]{2,1,0:T(8,128)}, s32[]{:T(128)}, s32[32]{0:T(128)S(1)}, s32[]{:T(128)}, /*index=5*/bf16[32,128,128]{2,1,0:T(8,128)(...) while((s32[]{:T(128)}, f32[4,1024,512]{2,1,0:T(8,128)}, ...), condition=%wide.region_5.6_spmd, body=%wide.region_4.5_spmd.sunk | while | flops 270532640 | bytes 19138228 | solution.py:49
  246.7 1.7 fusion.394
  248.4 1.7 fusion.395
  252.3 1.7 fusion.396
  257.8 1.7 fusion.398
  265.2 1.7 fusion.401
  270.7 1.7 fusion.403
  274.5 1.7 fusion.404
  280.1 1.7 fusion.406
  281.8 1.7 fusion.407
  285.6 1.7 fusion.408
  287.3 1.7 fusion.409
  289.0 8.7 %copy.13 = f32[4,1024,512]{1,2,0:T(8,128)} copy(f32[4,1024,512]{2,1,0:T(8,128)} %get-tuple-element.334) | data formatting | bytes 16777216 | tf_op jit(solution)/shard_map/while | solution.py:49
  297.7 5.0 fusion.193
  303.4 3.5 add_bitcast_fusion
  307.0 3.2 slice_bitcast_fusion.48
  310.3 365.0 %all-reduce.3.cloned.1.call-done = f32[3,512,512]{1,2,0:T(8,128)} async-done(((f32[3,512,512]{1,2,0:T(8,128)}), f32[3,512,512]{1,2,0:T(8,128)}) %all-reduce.3.cloned.1.call-update) | async-done | bytes 3145744 | tf_op jit(solution)/shard_map/psum | solution.py:83
  675.3 38.2 %reduce-scatter.2.cloned.1.call-done = f32[128,512]{1,0:T(8,128)} async-done(((f32[1024,512]{1,0:T(8,128)}), f32[128,512]{1,0:T(8,128)}) %reduce-scatter.2.cloned.1.call-update) | async-done | bytes 262160 | tf_op jit(solution)/shard_map/reduce_scatter | solution.py:76
  715.1 86.9 %all-reduce.5.cloned.1.call-done = f32[3,512,512]{1,2,0:T(8,128)} async-done(((f32[3,512,512]{1,2,0:T(8,128)}), f32[3,512,512]{1,2,0:T(8,128)}) %all-reduce.5.cloned.1.call-update) | async-done | bytes 3145744 | tf_op jit(solution)/shard_map/psum | solution.py:84
  802.0 3.5 copy.14
  (103 shorter events, 103.5 us)
Async XLA Ops:
  7.2 290.5 %all-gather.2.cloned.1.call-start = ((), (), s32[]{:S(2)}) async-start(), calls=%async_computation.2 | async-start | bytes 1179648 | tf_op jit(solution)/shard_map/all_gather | solution.py:78
  7.9 667.4 %all-reduce.3.cloned.1.call-start = ((), (), s32[]{:S(2)}) async-start(), calls=%async_computation.3 | async-start | bytes 6291456 | tf_op jit(solution)/shard_map/psum | solution.py:83
  23.9 10.1 %copy-start.1 = (s32[3,1,1,32]{3,2,1,0:T(1,128)S(1)}, s32[3,1,1,32]{3,2,1,0:T(1,128)}, u32[]{:S(2)}) copy-start(s32[3,1,1,32]{3,2,1,0:T(1,128)} %param.17) | copy-start | bytes 1156
  23.9 10.0 %copy-start.2 = (s32[3,1,1,32]{3,2,1,0:T(1,128)S(1)}, s32[3,1,1,32]{3,2,1,0:T(1,128)}, u32[]{:S(2)}) copy-start(s32[3,1,1,32]{3,2,1,0:T(1,128)} %param.18) | copy-start | bytes 1156
  297.7 5.5 copy-start
  297.7 5.7 copy-start.3
  306.9 406.6 %reduce-scatter.2.cloned.1.call-start = ((), (), s32[]{:S(2)}) async-start(), calls=%async_computation.1 | async-start | bytes 2359296 | tf_op jit(solution)/shard_map/reduce_scatter | solution.py:76
  310.2 491.8 %all-reduce.5.cloned.1.call-start = ((), (), s32[]{:S(2)}) async-start(), calls=%async_computation.4 | async-start | bytes 6291456 | tf_op jit(solution)/shard_map/psum | solution.py:84
Sparse Core Ops, SparseCore 0:
  9.6 24.9 all-gather.1
  307.0 368.1 all-reduce.2
  677.6 35.9 reduce-scatter.1
  716.5 85.5 all-reduce.4
